TPU v7x, 32 devices: a whole 2x2x4 slice. The times are simulated.
32 devices in a mesh: dp: 4 (over x, core), context: 2 (over y), tensor: 4 (over z).
Axes of the slice: x: 2, y: 2, z: 4, core: 2. Of those that a mesh axis runs over, the one named last changes fastest.
Arguments:
- tokens: bfloat16 [12, 512, 1536], P('dp', 'context')
- cotangent: bfloat16 [12, 512, 1536], P('dp', 'context'), may hold values from -6 to 6
- segments: int32 [12, 512], P('dp'), may hold values from 0 to 3, as said below
- positions: int32 [12, 512], P('dp', 'context'), may hold values from 0 to 255, as said below
- norm_attn: bfloat16 [1536], replicated, may hold values from 0.099609375 to 1.8984375
- w_query: bfloat16 [1536, 1536], P(None, 'tensor')
- key_weight: bfloat16 [1536, 768], P(None, 'tensor')
- value_weight: bfloat16 [1536, 768], P(None, 'tensor'), may hold values from -0.15625 to 0.15625
- w_out: bfloat16 [1536, 1536], P('tensor'), may hold values from -0.875 to 0.875
- norm_ffn: bfloat16 [1536], replicated, may hold values from 0.099609375 to 1.8984375
- w_gate: bfloat16 [1536, 4096], P(None, 'tensor'), may hold values from -0.15625 to 0.15625
- w_up: bfloat16 [1536, 4096], P(None, 'tensor'), may hold values from -0.15625 to 0.15625
- w_down: bfloat16 [4096, 1536], P('tensor'), may hold values from -0.09375 to 0.09375
Outputs:
- block_out: bfloat16 [12, 512, 1536], P('dp', 'context')
- input_grad: bfloat16 [12, 512, 1536], P('dp', 'context')
- attn_gain_grad: float32 [1536], replicated
- query_grad: float32 [1536, 1536], P(None, 'tensor')
- key_grad: float32 [1536, 768], P(None, 'tensor')
- value_grad: float32 [1536, 768], P(None, 'tensor')
- out_grad: float32 [1536, 1536], P('tensor')
- ffn_gain_grad: float32 [1536], replicated
- gate_grad: float32 [1536, 4096], P(None, 'tensor')
- up_grad: float32 [1536, 4096], P(None, 'tensor')
- down_grad: float32 [4096, 1536], P('tensor')
Inputs may be any that keep to these rules, and one draw needn't show every extreme that they name: `segments`: each sequence holds exactly four documents, numbered from 0 on its first token, never falling and rising by one at the first token of each further document; one of the four is 256 tokens long and the others are shorter. `positions`: each token's position is its offset from the first token of its document in its sequence.
All inputs are finite; a program needn't handle non-finite values.
Results may differ from a plain program's by a relative error of at most 0.019.
Values may be sent and summed in bfloat16 or wider, within the bound.
A program may use at most 192 MiB of HBM per device.

v0:
```python
import math
import jax
import jax.numpy as jnp
from jax import lax
from jax.sharding import PartitionSpec as P

HEAD_SIZE = 96
EPS = 1e-05
THETA = 100000.0
NEG_LARGE = -1e30


def shifted(x, axis, by):
    peers = lax.axis_size(axis)
    pairs = [(i, i + by) for i in range(peers) if 0 <= i + by < peers]
    return lax.ppermute(x, axis, pairs)


def rope_tables(position_rows):
    steps_half = jnp.arange(HEAD_SIZE // 2).astype(jnp.float32)
    inverse = THETA ** (-2.0 * steps_half / HEAD_SIZE)
    angles = position_rows.astype(jnp.float32)[..., None] * inverse
    return (jnp.cos(angles), jnp.sin(angles))


def apply_rotary(operand, cosine, sine_part):
    half_width = operand.shape[-1] // 2
    lead_half = operand[..., :half_width]
    tail_half = operand[..., half_width:]
    return jnp.concatenate(
        [lead_half * cosine - tail_half * sine_part, tail_half * cosine + lead_half * sine_part],
        axis=-1,
    )


def inverse_rotary(operand, cosine, sine_part):
    half_width = operand.shape[-1] // 2
    lead_half = operand[..., :half_width]
    tail_half = operand[..., half_width:]
    return jnp.concatenate(
        [lead_half * cosine + tail_half * sine_part, tail_half * cosine - lead_half * sine_part],
        axis=-1,
    )


def dot_wide(left_side, right_side):
    return jnp.dot(left_side, right_side, preferred_element_type=jnp.float32)


def on_device(
    tokens,
    cotangent,
    segments,
    positions,
    norm_attn,
    w_query,
    key_weight,
    value_weight,
    w_out,
    norm_ffn,
    w_gate,
    w_up,
    w_down,
):
    single_float = jnp.float32
    brain_float_half = jnp.bfloat16
    seq_count, slice_len, model_width = tokens.shape
    seq_length = segments.shape[1]
    row_count = seq_count * slice_len
    query_width = w_query.shape[1]
    pair_width = key_weight.shape[1]
    kv_heads = pair_width // HEAD_SIZE
    group_of_head = query_width // HEAD_SIZE // kv_heads
    key_block = min(512, seq_length)
    score_scale = 1.0 / math.sqrt(HEAD_SIZE)
    my_slice = lax.axis_index("context")
    first_row = my_slice * slice_len
    query_seg = lax.dynamic_slice_in_dim(segments, first_row, slice_len, 1)
    query_index = first_row + jnp.arange(slice_len, dtype=jnp.int32)
    block_count = (first_row + slice_len + key_block - 1) // key_block
    tok_flat = tokens.reshape(row_count, model_width).astype(single_float)
    inv_attn = lax.rsqrt(jnp.mean(tok_flat * tok_flat, axis=-1, keepdims=True) + EPS)
    normalized_attention_input = (tok_flat * inv_attn * norm_attn.astype(single_float)).astype(
        brain_float_half
    )
    cosine, sine_part = rope_tables(positions)
    cos_query = cosine[:, :, None, None, :]
    sin_query = sine_part[:, :, None, None, :]
    cos_key = cosine[:, :, None, :]
    sin_key = sine_part[:, :, None, :]
    query_rows = apply_rotary(
        dot_wide(normalized_attention_input, w_query).reshape(
            seq_count, slice_len, kv_heads, group_of_head, HEAD_SIZE
        ),
        cos_query,
        sin_query,
    ).astype(brain_float_half)
    keys_local = apply_rotary(
        dot_wide(normalized_attention_input, key_weight).reshape(
            seq_count, slice_len, kv_heads, HEAD_SIZE
        ),
        cos_key,
        sin_key,
    ).astype(brain_float_half)
    values_local = dot_wide(normalized_attention_input, value_weight).astype(brain_float_half)
    pair_local = jnp.concatenate(
        [
            keys_local.reshape(seq_count, slice_len, pair_width),
            values_local.reshape(seq_count, slice_len, pair_width),
        ],
        axis=-1,
    )
    pair_all = lax.all_gather(pair_local, "context", axis=1, tiled=True)

    def score_block(pair_source, start_key):
        piece = lax.dynamic_slice_in_dim(pair_source, start_key, key_block, 1)
        key_part = piece[..., :pair_width].reshape(seq_count, key_block, kv_heads, HEAD_SIZE)
        value_part = piece[..., pair_width:].reshape(seq_count, key_block, kv_heads, HEAD_SIZE)
        scores = (
            jnp.einsum(
                "sigrd,sjgd->sgrij", query_rows, key_part, preferred_element_type=single_float
            )
            * score_scale
        )
        key_seg = lax.dynamic_slice_in_dim(segments, start_key, key_block, 1)
        key_index = start_key + jnp.arange(key_block, dtype=jnp.int32)
        allowed = (key_seg[:, None, :] == query_seg[:, :, None]) & (
            key_index[None, None, :] <= query_index[None, :, None]
        )
        return (scores, allowed[:, None, None, :, :], key_part, value_part)

    def stats_step(index_block, carry):
        run_max, run_sum = carry
        scores, allowed, key_part, value_part = score_block(pair_all, index_block * key_block)
        masked = jnp.where(allowed, scores, NEG_LARGE)
        new_max = jnp.maximum(run_max, jnp.max(masked, axis=-1))
        block_sum = jnp.sum(jnp.where(allowed, jnp.exp(masked - new_max[..., None]), 0.0), axis=-1)
        return (new_max, run_sum * jnp.exp(run_max - new_max) + block_sum)

    stat_shape = (seq_count, kv_heads, group_of_head, slice_len)
    run_max, run_sum = lax.fori_loop(
        0,
        block_count,
        stats_step,
        (jnp.full(stat_shape, NEG_LARGE, single_float), jnp.zeros(stat_shape, single_float)),
    )
    log_total = run_max + jnp.log(run_sum)

    def output_step(index_block, accum):
        scores, allowed, key_part, value_part = score_block(pair_all, index_block * key_block)
        probs = jnp.where(allowed, jnp.exp(scores - log_total[..., None]), 0.0).astype(
            brain_float_half
        )
        return accum + jnp.einsum(
            "sgrij,sjgd->sigrd", probs, value_part, preferred_element_type=single_float
        )

    attn_accum = lax.fori_loop(
        0,
        block_count,
        output_step,
        jnp.zeros((seq_count, slice_len, kv_heads, group_of_head, HEAD_SIZE), single_float),
    )
    attended = attn_accum.astype(brain_float_half).reshape(row_count, query_width)
    attn_total = lax.psum(dot_wide(attended, w_out).astype(jnp.bfloat16), "tensor").astype(
        jnp.float32
    )
    hidden_res = tok_flat + attn_total
    inv_ffn = lax.rsqrt(jnp.mean(hidden_res * hidden_res, axis=-1, keepdims=True) + EPS)
    normed_ffn = (hidden_res * inv_ffn * norm_ffn.astype(single_float)).astype(brain_float_half)
    gate_proj = dot_wide(normed_ffn, w_gate)
    up_proj = dot_wide(normed_ffn, w_up)
    sigmoid_gate = jax.nn.sigmoid(gate_proj)
    silu_gate = gate_proj * sigmoid_gate
    activated = (silu_gate * up_proj).astype(brain_float_half)
    ffn_total = lax.psum(dot_wide(activated, w_down).astype(jnp.bfloat16), "tensor").astype(
        jnp.float32
    )
    block_out = (
        (hidden_res + ffn_total).astype(brain_float_half).reshape(seq_count, slice_len, model_width)
    )
    grad_rows = cotangent.reshape(row_count, model_width)
    down_grad = dot_wide(activated.T, grad_rows)
    grad_act = dot_wide(grad_rows, w_down.T)
    grad_gate = (
        grad_act * up_proj * sigmoid_gate * (1.0 + gate_proj * (1.0 - sigmoid_gate))
    ).astype(brain_float_half)
    grad_up = (grad_act * silu_gate).astype(brain_float_half)
    gate_grad = dot_wide(normed_ffn.T, grad_gate)
    up_grad = dot_wide(normed_ffn.T, grad_up)
    grad_normed_ffn = lax.psum(
        (dot_wide(grad_gate, w_gate.T) + dot_wide(grad_up, w_up.T)).astype(jnp.bfloat16), "tensor"
    ).astype(jnp.float32)
    ffn_gain_grad = jnp.sum(grad_normed_ffn * hidden_res * inv_ffn, axis=0)
    scaled_ffn = grad_normed_ffn * norm_ffn.astype(single_float)
    grad_hidden = (
        grad_rows.astype(single_float)
        + inv_ffn * scaled_ffn
        - hidden_res * inv_ffn**3 * jnp.mean(scaled_ffn * hidden_res, axis=-1, keepdims=True)
    )
    grad_hidden_b = grad_hidden.astype(brain_float_half)
    out_grad = dot_wide(attended.T, grad_hidden_b)
    attended_gradient = (
        dot_wide(grad_hidden_b, w_out.T)
        .astype(brain_float_half)
        .reshape(seq_count, slice_len, kv_heads, group_of_head, HEAD_SIZE)
    )
    attended_heads = attended.reshape(seq_count, slice_len, kv_heads, group_of_head, HEAD_SIZE)
    row_delta = jnp.sum(
        attended_gradient.astype(single_float) * attended_heads.astype(single_float), axis=-1
    )
    delta_heads = jnp.transpose(row_delta, (0, 2, 3, 1))

    def grad_step(index_block, carry):
        query_accum, pair_accum = carry
        start_key = index_block * key_block
        scores, allowed, key_part, value_part = score_block(pair_all, start_key)
        weights = jnp.where(allowed, jnp.exp(scores - log_total[..., None]), 0.0)
        prob_grad = jnp.einsum(
            "sigrd,sjgd->sgrij", attended_gradient, value_part, preferred_element_type=single_float
        )
        score_grad = (weights * (prob_grad - delta_heads[..., None]) * score_scale).astype(
            brain_float_half
        )
        query_accum = query_accum + jnp.einsum(
            "sgrij,sjgd->sigrd", score_grad, key_part, preferred_element_type=single_float
        )
        key_term = jnp.einsum(
            "sgrij,sigrd->sjgd", score_grad, query_rows, preferred_element_type=single_float
        )
        value_term = jnp.einsum(
            "sgrij,sigrd->sjgd",
            weights.astype(brain_float_half),
            attended_gradient,
            preferred_element_type=single_float,
        )
        both_terms = jnp.concatenate(
            [
                key_term.reshape(seq_count, key_block, pair_width),
                value_term.reshape(seq_count, key_block, pair_width),
            ],
            axis=-1,
        )
        current = lax.dynamic_slice_in_dim(pair_accum, start_key, key_block, 1)
        pair_accum = lax.dynamic_update_slice_in_dim(pair_accum, current + both_terms, start_key, 1)
        return (query_accum, pair_accum)

    query_accum, pair_accum = lax.fori_loop(
        0,
        block_count,
        grad_step,
        (
            jnp.zeros((seq_count, slice_len, kv_heads, group_of_head, HEAD_SIZE), single_float),
            jnp.zeros((seq_count, seq_length, 2 * pair_width), single_float),
        ),
    )
    slice_count = lax.axis_size("context")

    def owner_step(turn, incoming):
        owner = my_slice + turn - (slice_count - 1)
        own_rows = lax.dynamic_slice_in_dim(
            pair_accum, jnp.maximum(owner, 0) * slice_len, slice_len, 1
        )
        message = jnp.where(owner >= 0, incoming + own_rows, 0.0)
        return shifted(message, "context", -1)

    arrived = lax.fori_loop(
        0,
        slice_count - 1,
        owner_step,
        jnp.zeros((seq_count, slice_len, 2 * pair_width), single_float),
    )
    pair_grad = arrived + lax.dynamic_slice_in_dim(pair_accum, first_row, slice_len, 1)
    key_linear = (
        inverse_rotary(
            pair_grad[..., :pair_width].reshape(seq_count, slice_len, kv_heads, HEAD_SIZE),
            cos_key,
            sin_key,
        )
        .astype(brain_float_half)
        .reshape(row_count, pair_width)
    )
    value_linear = (
        pair_grad[..., pair_width:].astype(brain_float_half).reshape(row_count, pair_width)
    )
    query_lin = (
        inverse_rotary(query_accum, cos_query, sin_query)
        .astype(brain_float_half)
        .reshape(row_count, query_width)
    )
    query_grad = dot_wide(normalized_attention_input.T, query_lin)
    key_grad = dot_wide(normalized_attention_input.T, key_linear)
    value_grad = dot_wide(normalized_attention_input.T, value_linear)
    back_attn = (
        dot_wide(query_lin, w_query.T)
        + dot_wide(key_linear, key_weight.T)
        + dot_wide(value_linear, value_weight.T)
    )
    grad_normed_attn = lax.psum(back_attn.astype(jnp.bfloat16), "tensor").astype(jnp.float32)
    attn_gain_grad = jnp.sum(grad_normed_attn * tok_flat * inv_attn, axis=0)
    scaled_attn = grad_normed_attn * norm_attn.astype(single_float)
    input_grad = (
        grad_hidden
        + inv_attn * scaled_attn
        - tok_flat * inv_attn**3 * jnp.mean(scaled_attn * tok_flat, axis=-1, keepdims=True)
    )
    input_grad = input_grad.astype(brain_float_half).reshape(seq_count, slice_len, model_width)
    all_sums = lax.psum(
        (
            attn_gain_grad,
            query_grad,
            key_grad,
            value_grad,
            out_grad,
            ffn_gain_grad,
            gate_grad,
            up_grad,
            down_grad,
        ),
        ("dp", "context"),
    )
    return (
        block_out,
        input_grad,
        all_sums[0],
        all_sums[1],
        all_sums[2],
        all_sums[3],
        all_sums[4],
        all_sums[5],
        all_sums[6],
        all_sums[7],
        all_sums[8],
    )


def solution(mesh):
    placed = (
        P("dp", "context", None),
        P("dp", "context", None),
        P("dp", None),
        P("dp", "context"),
        P(),
        P(None, "tensor"),
        P(None, "tensor"),
        P(None, "tensor"),
        P("tensor", None),
        P(),
        P(None, "tensor"),
        P(None, "tensor"),
        P("tensor", None),
    )
    return jax.shard_map(
        on_device,
        mesh=mesh,
        in_specs=placed,
        out_specs=(
            P("dp", "context", None),
            P("dp", "context", None),
            P(),
            P(None, "tensor"),
            P(None, "tensor"),
            P(None, "tensor"),
            P("tensor", None),
            P(),
            P(None, "tensor"),
            P(None, "tensor"),
            P("tensor", None),
        ),
        check_vma=False,
    )
```

profile of v0, /device:TPU:0, one launch (start us, length us, event | category | flops | bytes accessed | tf_op | source)
XLA Modules:
  0.0 889.8 jit_solution(11171474708792457560)
XLA Ops:
  10.4 2.3 fusion.52
  20.0 2.5 pad_maximum_fusion
  22.6 2.4 copy.51
  25.0 3.1 fusion.57
  29.1 23.4 %all-gather.2.cloned.1.call-done = bf16[3,512,384]{1,0,2:T(4,128)(2,1)} async-done(((bf16[3,256,384]{1,0,2:T(4,128)(2,1)}), bf16[3,512,384]{1,0,2:T(4,128)(2,1)}) %all-gather.2.cloned.1.call-update) | async-done | bytes 1179664 | tf_op jit(solution)/shard_map/all_gather | solution.py:113
  52.6 2.7 copy.53
  55.3 5.6 while.42
  62.6 7.8 while.43
  63.1 2.4 fusion.162
  65.5 4.7 fusion.163
  70.4 3.3 copy.54
  73.7 3.3 reshape.332
  77.0 4.2 convolution_convert_fusion.1
  81.9 94.1 %all-reduce.8.cloned.1.call-done = bf16[768,1536]{1,0:T(8,128)(2,1)} async-done(((bf16[768,1536]{1,0:T(8,128)(2,1)}), bf16[768,1536]{1,0:T(8,128)(2,1)}) %all-reduce.8.cloned.1.call-update) | async-done | bytes 2359312 | tf_op jit(solution)/shard_map/psum | solution.py:165
  176.0 3.4 multiply_reduce_fusion
  181.7 2.6 fusion.70
  184.4 2.6 fusion.69
  187.1 5.0 multiply_convert_fusion.1
  192.0 2.6 fusion.71
  194.7 4.0 add_convert_fusion.1
  198.9 93.6 %all-reduce.10.cloned.1.call-done = bf16[768,1536]{1,0:T(8,128)(2,1)} async-done(((bf16[768,1536]{1,0:T(8,128)(2,1)}), bf16[768,1536]{1,0:T(8,128)(2,1)}) %all-reduce.10.cloned.1.call-update) | async-done | bytes 2359312 | tf_op jit(solution)/shard_map/psum | solution.py:191
  292.5 5.0 fusion.47
  297.7 3.5 fusion.44
  305.5 3.7 reshape.335
  309.2 4.4 multiply_reduce_fusion.1
  313.6 3.0 copy.56
  320.8 12.2 %while.44 = (s32[]{:T(128)}, f32[3,256,2,2,96]{1,4,3,2,0:T(8,128)}, f32[3,512,384]{1,2,0:T(8,128)}, s32[]{:T(128)}, s32[3,512]{1,0:T(4,128)S(1)}, /*index=5*/s32...) while((s32[]{:T(128)}, f32[3,256,2,2,96]{1,4,3,2,0:T(8,128)}, ...), condition=%wide.region_14.15_spmd.clone, body=%wide.region_13.14_spmd.clone.sunk | while | flops 1529643776 | bytes 81120576 | solution.py:248
  325.6 2.5 fusion.176
  333.0 2.5 dynamic-slice_select_fusion
  336.8 3.8 convolution_convert_fusion
  341.7 3.0 copy.58
  344.7 3.3 convert_element_type.180
  348.0 3.0 fusion.72
  351.0 14.2 %collective-permute-done = f32[3,256,384]{1,2,0:T(8,128)} collective-permute-done((f32[3,256,384]{1,2,0:T(8,128)}, f32[3,256,384]{1,2,0:T(8,128)}, u32[]{:S(2)}, u32[]{:S(2)}) %collective-permute-start) | collective-permute-done | bytes 1179680 | tf_op jit(solution)/shard_map/while/body/eval_jaxpr/ppermute | solution.py:16
  371.8 7.6 fusion.77
  379.5 4.6 fusion.76
  384.1 4.6 fusion.75
  388.6 2.8 fusion.74
  391.5 2.6 fusion.61
  398.0 144.0 %all-reduce.14.cloned.1.call-done = (bf16[768,1536]{1,0:T(8,128)(2,1)}, bf16[768,1536]{1,0:T(8,128)(2,1)}) async-done(((bf16[768,1536]{1,0:T(8,128)(2,1)}, bf16[768,1536]{1,0:T(8,128)(2,1)}), (bf16[768,1536]{1,0:T(8,128)(2,1)}, bf16[768,1536]{1,0:T(8,128)(2,1)})) %all-reduce.14.cloned.1.call-update) | async-done | bytes 4718608 | tf_op jit(solution)/shard_map/psum | solution.py:176
  542.0 4.1 fusion.49
  546.1 25.9 %all-reduce = (f32[1536]{0:T(1024)}, f32[1536]{0:T(1024)}) all-reduce(f32[1536]{0:T(1024)S(1)} %get-tuple-element.347, f32[1536]{0:T(1024)S(1)} %get-tuple-element.345), channel_id=1, replica_groups=mesh['dp'=4,'context'=2,'tensor'=4] {'dp','context'}, use_global_device_ids=true, to_apply=%region_18.19 | all-reduce | flops 3072 | bytes 24576 | tf_op jit(solution)/shard_map/psum | solution.py:308
  572.0 8.9 %fusion.41 = (bf16[768,1536]{1,0:T(8,128)(2,1)}, bf16[768,1536]{1,0:T(8,128)(2,1)}) fusion(f32[768,1536]{1,0:T(8,128)} %copy-done.8, bf16[768,1536]{1,0:T(8,128)(2,1)} %get-tuple-element.419, bf16[3,256,1536]{2,1,0:T(8,128)(2,1)} %param.19, f32[768]{0:T(1024)S(1)} %broadcast_multiply_fusion, f32[768]{0:T(1024)S(1)} %multiply_multiply_fusion, ...), kind=kLoop, calls=%fused_computation.55 | loop fusion | flops 16515072 | bytes 18889728 | tf_op jit(solution)/shard_map/convert_element_type | solution.py:307
  581.0 282.7 %all-reduce.12.cloned.1.call-done = (f32[1536,384]{1,0:T(8,128)}, f32[1536,192]{0,1:T(8,128)}, f32[1536,192]{0,1:T(8,128)}, f32[384,1536]{1,0:T(8,128)}, f32[153...) async-done(((f32[1536,384]{1,0:T(8,128)}, f32[1536,192]{0,1:T(8,128)}, f32[1536,192]{0,1:T(8,128)}, f32[384,1536]{1,0:T(8,128)}, f32[1536,1024]{1,0:T(8,128)}, ...) | async-done | bytes 25952272 | tf_op jit(solution)/shard_map/psum | solution.py:308
  863.6 3.4 copy.112
  872.4 3.2 copy.116
  875.8 3.2 copy.117
  880.4 2.7 copy.118
  (204 shorter events, 60.4 us)
Async XLA Ops:
  7.2 179.9 %copy-start = (bf16[1024,1536]{1,0:T(8,128)(2,1)S(1)}, bf16[1024,1536]{1,0:T(8,128)(2,1)}, u32[]{:S(2)}) copy-start(bf16[1024,1536]{1,0:T(8,128)(2,1)} %param.31) | copy-start | bytes 9437188
  7.2 3.2 copy-start.44
  7.2 45.4 %all-gather.2.cloned.1.call-start = ((), (), s32[]{:S(2)}) async-start(), calls=%async_computation | async-start | bytes 2359296 | tf_op jit(solution)/shard_map/all_gather | solution.py:113
  10.4 5.1 copy-start.41
  10.4 5.1 copy-start.39
  10.4 3.0 copy-start.26
  13.4 14.7 %copy-start.21 = (f32[3,256,48]{1,2,0:T(8,128)}, f32[3,256,48]{1,2,0:T(8,128)S(1)}, u32[]{:S(2)}) copy-start(f32[3,256,48]{1,2,0:T(8,128)S(1)} %get-tuple-element.439) | copy-start | bytes 442372
  13.4 14.7 %copy-start.23 = (f32[3,256,48]{1,2,0:T(8,128)}, f32[3,256,48]{1,2,0:T(8,128)S(1)}, u32[]{:S(2)}) copy-start(f32[3,256,48]{1,2,0:T(8,128)S(1)} %get-tuple-element.440) | copy-start | bytes 442372
  20.0 5.0 copy-start.32
  22.5 153.5 %all-reduce.8.cloned.1.call-start = ((), (), s32[]{:S(2)}) async-start(), calls=%async_computation.1 | async-start | bytes 4718592 | tf_op jit(solution)/shard_map/psum | solution.py:165
  81.2 211.3 %all-reduce.10.cloned.1.call-start = ((), (), s32[]{:S(2)}) async-start(), calls=%async_computation.2 | async-start | bytes 4718592 | tf_op jit(solution)/shard_map/psum | solution.py:191
  176.0 3.4 copy-start.2
  176.0 3.8 copy-start.9
  181.7 2.6 copy-start.30
  181.7 2.7 copy-start.46
  184.4 2.6 copy-start.28
  192.0 2.6 copy-start.49
  192.0 2.7 copy-start.51
  198.7 343.4 %all-reduce.14.cloned.1.call-start = ((), (), s32[]{:S(2)}) async-start(), calls=%async_computation.4 | async-start | bytes 9437184 | tf_op jit(solution)/shard_map/psum | solution.py:176
  292.5 5.0 copy-start.3
  292.5 5.0 copy-start.10
  292.5 5.2 copy-start.16
  297.7 5.7 copy-start.33
  316.6 4.2 copy-start.43
  333.0 3.8 copy-start.48
  335.5 29.7 %collective-permute-start = (f32[3,256,384]{1,2,0:T(8,128)}, f32[3,256,384]{1,2,0:T(8,128)}, u32[]{:S(2)}, u32[]{:S(2)}) collective-permute-start(f32[3,256,384]{1,2,0:T(8,128)} %dynamic-slice_select_fusion), channel_id=1, source_target_pairs={{4,0},{5,1},{6,2},{7,3},{12,8},{13,9},{14,10},{15,11},{20,16},{21,... | collective-permute-start | bytes 3538952 | tf_op jit(solution)/shard_map/while/body/eval_jaxpr/ppermute | solution.py:16
  336.8 3.9 copy-start.13
  336.8 3.9 copy-start.22
  336.8 3.8 copy-start.24
  348.0 17.3 %copy-start.7 = (f32[3,512,384]{1,2,0:T(8,128)S(1)}, f32[3,512,384]{1,2,0:T(8,128)}, u32[]{:S(2)}) copy-start(f32[3,512,384]{1,2,0:T(8,128)} %get-tuple-element.191) | copy-start | bytes 7077892
  371.6 492.1 %all-reduce.12.cloned.1.call-start = ((), (), s32[]{:S(2)}) async-start(), calls=%async_computation.3 | async-start | bytes 51904512 | tf_op jit(solution)/shard_map/psum | solution.py:308
  371.8 7.7 copy-start.31
  371.8 7.7 copy-start.52
  379.5 4.6 copy-start.50
  379.5 12.0 %slice-start = ((s8[4718592]{0:T(1024)(128)(4,1)}), s8[4194304]{0:T(1024)(128)(4,1)S(1)}, s32[]{:S(2)}) async-start(s8[4718592]{0:T(1024)(128)(4,1)} %bitcast.261), calls=%async_computation.5 | async-start | bytes 8388608
  384.1 4.6 copy-start.15
  384.1 4.6 copy-start.20
  384.1 7.4 slice-start.1
  388.6 2.8 copy-start.25
  391.5 2.6 copy-start.19
  397.4 144.7 %copy-start.40 = (f32[1536]{0:T(1024)S(1)}, f32[1536]{0:T(1024)}, u32[]{:S(2)}) copy-start(f32[1536]{0:T(1024)} %copy-done.39) | copy-start | bytes 18436
  863.6 3.4 copy-start.35
  863.6 4.4 copy-start.34
  868.0 4.3 copy-start.17
  869.3 6.2 slice-start.4
  872.4 3.4 slice-start.5
  872.4 7.0 slice-start.2
  875.8 4.6 slice-start.3
  (17 other events, 26.1 us)
Sparse Core Ops, SparseCore 0:
  22.7 29.8 all-gather.1
  81.3 94.6 all-reduce.7
  198.8 93.6 all-reduce.9
  371.7 170.3 all-reduce.13
  548.2 315.3 all-reduce.11
where the time goes:
time: 899 us; the launch traced here: 890 us
  waiting for transfers between devices  652 us (73%)
  matrix products  78 us (9%)
  local copies, waits for them, and re-layouts  66.8 us (7%)
  other arithmetic  49.9 us (6%)
  blocking collectives  25.9 us (3%)
  between operations  14.5 us (2%)
    psum x1, waiting for transfers between devices, on_device(): lax.psum((attn_gain_grad, query_grad, key_grad, value_grad, out_grad, ffn...  283 us
    psum x1, waiting for transfers between devices, on_device(): lax.psum(dot_wide(activated, w_down).astype(jnp.bfloat16), 'tensor')  144 us
    psum x1, waiting for transfers between devices, on_device(): lax.psum(dot_wide(attended, w_out).astype(jnp.bfloat16), 'tensor')  94.1 us
    psum x1, waiting for transfers between devices, on_device(): lax.psum((dot_wide(grad_gate, w_gate.T) + dot_wide(grad_up, w_up.T)).asty...  93.6 us
    dot_general x21, matrix products, dot_wide(): return jnp.dot(left_side, right_side, preferred_element_type=jnp.float32)  64.1 us
    unnamed x119, local copies, waits for them, and re-layouts  35.9 us
    psum x1, blocking collectives, on_device(): lax.psum((attn_gain_grad, query_grad, key_grad, value_grad, out_grad, ffn...  25.9 us
    all_gather x1, waiting for transfers between devices, on_device(): pair_all = lax.all_gather(pair_local, 'context', axis=1, tiled=True)  23.4 us
  transfers between devices with their start and end apart: 6, of which 6 were waited for; matrix products, arithmetic and copies ran while one was open for 7% of the time, Pallas kernels for 0%

commit v1 on v0

--- a/solution.py
+++ b/solution.py
@@ -173,7 +173,10 @@
     sigmoid_gate = jax.nn.sigmoid(gate_proj)
     silu_gate = gate_proj * sigmoid_gate
     activated = (silu_gate * up_proj).astype(brain_float_half)
-    ffn_total = lax.psum(dot_wide(activated, w_down).astype(jnp.bfloat16), "tensor").astype(
+    update_the_sheet = lambda incoming_x, link_axis: lax.all_gather(incoming_x, link_axis).sum(
+        axis=0
+    )
+    ffn_total = update_the_sheet(dot_wide(activated, w_down).astype(jnp.bfloat16), "tensor").astype(
         jnp.float32
     )
     block_out = (

time: 899 us -> 988 us (1.099)
  waiting for transfers between devices: 652 us -> 744 us
  local copies, waits for them, and re-layouts: 66.8 us -> 56.8 us
    all_gather x0 -> x1, waiting for transfers between devices: none -> 164 us  [on_device(): lax.all_gather(incoming_x, link_axis).sum(axis=0)]
    psum x1, waiting for transfers between devices: 144 us -> 70 us  [on_device(): lax.psum(back_attn.astype(jnp.bfloat16), 'tensor').astype(jnp.float32)]
    unnamed x119 -> x127, local copies, waits for them, and re-layouts: 35.9 us -> 36.3 us
  transfers between devices with their start and end apart: 6 -> 7, of which waited for: 6 -> 7; matrix products, arithmetic and copies ran while one was open for 7% -> 6% of each run, Pallas kernels for 0% -> 0%
where the time goes in v1:
time: 988 us; the launch traced here: 978 us
  waiting for transfers between devices  744 us (75%)
  matrix products  80.1 us (8%)
  local copies, waits for them, and re-layouts  56.8 us (6%)
  other arithmetic  53.3 us (5%)
  blocking collectives  25.9 us (3%)
  between operations  14.9 us (2%)
    psum x1, waiting for transfers between devices, on_device(): lax.psum((attn_gain_grad, query_grad, key_grad, value_grad, out_grad, ffn...  286 us
    all_gather x1, waiting for transfers between devices, on_device(): lax.all_gather(incoming_x, link_axis).sum(axis=0)  164 us
    psum x1, waiting for transfers between devices, on_device(): lax.psum(dot_wide(attended, w_out).astype(jnp.bfloat16), 'tensor')  94.1 us
    psum x1, waiting for transfers between devices, on_device(): lax.psum((dot_wide(grad_gate, w_gate.T) + dot_wide(grad_up, w_up.T)).asty...  88.2 us
    psum x1, waiting for transfers between devices, on_device(): lax.psum(back_attn.astype(jnp.bfloat16), 'tensor').astype(jnp.float32)  70 us
    dot_general x21, matrix products, dot_wide(): return jnp.dot(left_side, right_side, preferred_element_type=jnp.float32)  64.8 us
    unnamed x127, local copies, waits for them, and re-layouts  36.3 us
    psum x1, blocking collectives, on_device(): lax.psum((attn_gain_grad, query_grad, key_grad, value_grad, out_grad, ffn...  25.9 us
  transfers between devices with their start and end apart: 7, of which 7 were waited for; matrix products, arithmetic and copies ran while one was open for 6% of the time, Pallas kernels for 0%

profile of v1, /device:TPU:0, one launch (start us, length us, event | category | flops | bytes accessed | tf_op | source)
XLA Modules:
  0.0 978.2 jit_solution(1336034903707998716)
XLA Ops:
  10.4 2.3 fusion.52
  20.0 2.5 pad_maximum_fusion
  22.6 2.4 copy.51
  25.0 3.1 fusion.57
  29.1 23.4 %all-gather.4.cloned.1.call-done = bf16[3,512,384]{1,0,2:T(4,128)(2,1)} async-done(((bf16[3,256,384]{1,0,2:T(4,128)(2,1)}), bf16[3,512,384]{1,0,2:T(4,128)(2,1)}) %all-gather.4.cloned.1.call-update) | async-done | bytes 1179664 | tf_op jit(solution)/shard_map/all_gather | solution.py:113
  52.6 2.7 copy.53
  55.3 5.6 while.42
  56.9 2.3 fusion.157
  62.6 7.8 while.43
  63.1 2.4 fusion.162
  65.5 4.7 fusion.163
  70.4 3.3 copy.54
  73.7 3.3 reshape.332
  76.9 4.2 convolution_convert_fusion.1
  81.9 94.1 %all-reduce.7.cloned.1.call-done = bf16[768,1536]{1,0:T(8,128)(2,1)} async-done(((bf16[768,1536]{1,0:T(8,128)(2,1)}), bf16[768,1536]{1,0:T(8,128)(2,1)}) %all-reduce.7.cloned.1.call-update) | async-done | bytes 2359312 | tf_op jit(solution)/shard_map/psum | solution.py:165
  176.0 3.4 multiply_reduce_fusion
  181.7 2.6 fusion.70
  184.4 2.6 fusion.69
  187.0 5.0 multiply_convert_fusion.1
  192.0 2.6 fusion.71
  194.7 4.0 add_convert_fusion.1
  198.7 5.2 convolution_convert_fusion
  204.2 88.2 %all-reduce.9.cloned.1.call-done = bf16[768,1536]{1,0:T(8,128)(2,1)} async-done(((bf16[768,1536]{1,0:T(8,128)(2,1)}), bf16[768,1536]{1,0:T(8,128)(2,1)}) %all-reduce.9.cloned.1.call-update) | async-done | bytes 2359312 | tf_op jit(solution)/shard_map/psum | solution.py:194
  292.5 4.1 fusion.47
  296.6 163.7 %all-gather.6.cloned.1.call-done = bf16[3072,1536]{1,0:T(8,128)(2,1)} async-done(((bf16[768,1536]{1,0:T(8,128)(2,1)}), bf16[3072,1536]{1,0:T(8,128)(2,1)}) %all-gather.6.cloned.1.call-update) | async-done | bytes 9437200 | tf_op jit(solution)/shard_map/all_gather | solution.py:176
  460.3 7.2 reduce_sum.86
  467.5 6.8 fusion.44
  478.5 2.5 multiply_reduce_fusion.1
  485.9 11.5 %while.44 = (s32[]{:T(128)}, f32[3,256,2,2,96]{1,4,3,2,0:T(8,128)}, f32[3,512,384]{1,2,0:T(8,128)}, s32[]{:T(128)}, s32[3,512]{1,0:T(4,128)S(1)}, /*index=5*/s32...) while((s32[]{:T(128)}, f32[3,256,2,2,96]{1,4,3,2,0:T(8,128)}, ...), condition=%wide.region_14.15_spmd.clone, body=%wide.region_13.14_spmd.clone.sunk | while | flops 1529643776 | bytes 85839216 | solution.py:251
  489.5 2.4 fusion.176
  492.8 2.6 fusion.179
  497.5 2.5 dynamic-slice_select_fusion
  501.4 6.0 fusion.77
  508.8 2.9 fusion.72
  511.8 18.4 %collective-permute-done = f32[3,256,384]{1,2,0:T(8,128)} collective-permute-done((f32[3,256,384]{1,2,0:T(8,128)}, f32[3,256,384]{1,2,0:T(8,128)}, u32[]{:S(2)}, u32[]{:S(2)}) %collective-permute-start) | collective-permute-done | bytes 1179680 | tf_op jit(solution)/shard_map/while/body/eval_jaxpr/ppermute | solution.py:16
  538.2 6.4 fusion.76
  544.6 4.6 fusion.75
  549.2 2.8 fusion.74
  552.1 2.5 fusion.61
  558.6 70.0 %all-reduce.11.cloned.1.call-done = bf16[768,1536]{1,0:T(8,128)(2,1)} async-done(((bf16[768,1536]{1,0:T(8,128)(2,1)}), bf16[768,1536]{1,0:T(8,128)(2,1)}) %all-reduce.11.cloned.1.call-update) | async-done | bytes 2359312 | tf_op jit(solution)/shard_map/psum | solution.py:302
  628.6 3.4 fusion.49
  632.0 25.9 %all-reduce = (f32[1536]{0:T(1024)}, f32[1536]{0:T(1024)}) all-reduce(f32[1536]{0:T(1024)S(1)} %get-tuple-element.347, f32[1536]{0:T(1024)S(1)} %get-tuple-element.345), channel_id=1, replica_groups=mesh['dp'=4,'context'=2,'tensor'=4] {'dp','context'}, use_global_device_ids=true, to_apply=%region_18.19 | all-reduce | flops 3072 | bytes 24576 | tf_op jit(solution)/shard_map/psum | solution.py:311
  657.8 6.0 fusion.41
  663.8 286.4 %all-reduce.13.cloned.1.call-done = (f32[1536,384]{1,0:T(8,128)}, f32[1536,192]{0,1:T(8,128)}, f32[1536,192]{0,1:T(8,128)}, f32[384,1536]{1,0:T(8,128)}, f32[153...) async-done(((f32[1536,384]{1,0:T(8,128)}, f32[1536,192]{0,1:T(8,128)}, f32[1536,192]{0,1:T(8,128)}, f32[384,1536]{1,0:T(8,128)}, f32[1536,1024]{1,0:T(8,128)}, ...) | async-done | bytes 25952272 | tf_op jit(solution)/shard_map/psum | solution.py:311
  950.2 3.4 copy.111
  958.9 3.2 copy.115
  962.4 3.2 copy.116
  967.0 3.2 copy.117
  (218 shorter events, 57.9 us)
Async XLA Ops:
  7.2 179.9 %copy-start = (bf16[1024,1536]{1,0:T(8,128)(2,1)S(1)}, bf16[1024,1536]{1,0:T(8,128)(2,1)}, u32[]{:S(2)}) copy-start(bf16[1024,1536]{1,0:T(8,128)(2,1)} %param.31) | copy-start | bytes 9437188
  7.2 3.2 copy-start.51
  7.2 45.4 %all-gather.4.cloned.1.call-start = ((), (), s32[]{:S(2)}) async-start(), calls=%async_computation | async-start | bytes 2359296 | tf_op jit(solution)/shard_map/all_gather | solution.py:113
  10.4 5.1 copy-start.48
  10.4 5.1 copy-start.46
  10.4 3.0 copy-start.33
  13.4 14.7 %copy-start.26 = (f32[3,256,48]{1,2,0:T(8,128)}, f32[3,256,48]{1,2,0:T(8,128)S(1)}, u32[]{:S(2)}) copy-start(f32[3,256,48]{1,2,0:T(8,128)S(1)} %get-tuple-element.437) | copy-start | bytes 442372
  13.4 14.7 %copy-start.28 = (f32[3,256,48]{1,2,0:T(8,128)}, f32[3,256,48]{1,2,0:T(8,128)S(1)}, u32[]{:S(2)}) copy-start(f32[3,256,48]{1,2,0:T(8,128)S(1)} %get-tuple-element.438) | copy-start | bytes 442372
  20.0 5.0 copy-start.39
  22.5 153.5 %all-reduce.7.cloned.1.call-start = ((), (), s32[]{:S(2)}) async-start(), calls=%async_computation.1 | async-start | bytes 4718592 | tf_op jit(solution)/shard_map/psum | solution.py:165
  81.2 211.3 %all-reduce.9.cloned.1.call-start = ((), (), s32[]{:S(2)}) async-start(), calls=%async_computation.2 | async-start | bytes 4718592 | tf_op jit(solution)/shard_map/psum | solution.py:194
  176.0 3.4 copy-start.5
  176.0 3.8 copy-start.19
  181.7 2.7 copy-start.53
  192.0 2.6 copy-start.55
  192.0 2.7 copy-start.57
  198.6 261.6 %all-gather.6.cloned.1.call-start = ((), (), s32[]{:S(2)}) async-start(), calls=%async_computation.4 | async-start | bytes 11796480 | tf_op jit(solution)/shard_map/all_gather | solution.py:176
  203.9 88.5 %copy-start.6 = (bf16[3,256,1536]{2,1,0:T(8,128)(2,1)S(1)}, bf16[3,256,1536]{2,1,0:T(8,128)(2,1)}, u32[]{:S(2)}) copy-start(bf16[3,256,1536]{2,1,0:T(8,128)(2,1)} %param.19) | copy-start | bytes 7077892
  204.0 424.6 %all-reduce.11.cloned.1.call-start = ((), (), s32[]{:S(2)}) async-start(), calls=%async_computation.3 | async-start | bytes 4718592 | tf_op jit(solution)/shard_map/psum | solution.py:302
  467.5 9.0 copy-start.40
  482.7 3.2 copy-start.2
  482.7 3.2 copy-start.8
  482.7 3.2 copy-start.50
  497.5 4.0 copy-start.32
  500.0 7.4 copy-start.16
  500.0 7.4 copy-start.27
  500.0 7.4 copy-start.29
  500.0 30.2 %collective-permute-start = (f32[3,256,384]{1,2,0:T(8,128)}, f32[3,256,384]{1,2,0:T(8,128)}, u32[]{:S(2)}, u32[]{:S(2)}) collective-permute-start(f32[3,256,384]{1,2,0:T(8,128)} %dynamic-slice_select_fusion), channel_id=1, source_target_pairs={{4,0},{5,1},{6,2},{7,3},{12,8},{13,9},{14,10},{15,11},{20,16},{21,... | collective-permute-start | bytes 3538952 | tf_op jit(solution)/shard_map/while/body/eval_jaxpr/ppermute | solution.py:16
  508.8 3.0 copy-start.24
  508.8 21.4 %copy-start.12 = (f32[3,512,384]{1,2,0:T(8,128)S(1)}, f32[3,512,384]{1,2,0:T(8,128)}, u32[]{:S(2)}) copy-start(f32[3,512,384]{1,2,0:T(8,128)} %get-tuple-element.798) | copy-start | bytes 7077892
  536.5 413.7 %all-reduce.13.cloned.1.call-start = ((), (), s32[]{:S(2)}) async-start(), calls=%async_computation.5 | async-start | bytes 51904512 | tf_op jit(solution)/shard_map/psum | solution.py:311
  538.2 6.4 copy-start.38
  538.2 6.4 copy-start.56
  538.2 13.9 %slice-start = ((s8[4718592]{0:T(1024)(128)(4,1)}), s8[4194304]{0:T(1024)(128)(4,1)S(1)}, s32[]{:S(2)}) async-start(s8[4718592]{0:T(1024)(128)(4,1)} %bitcast.262), calls=%async_computation.6 | async-start | bytes 8388608
  544.6 4.6 copy-start.18
  544.6 4.6 copy-start.25
  544.6 7.4 slice-start.1
  549.2 2.8 copy-start.30
  557.9 70.7 %copy-start.7 = (bf16[3,256,1536]{2,1,0:T(8,128)(2,1)S(1)}, bf16[3,256,1536]{2,1,0:T(8,128)(2,1)}, u32[]{:S(2)}) copy-start(bf16[3,256,1536]{2,1,0:T(8,128)(2,1)} %param.19) | copy-start | bytes 7077892
  557.9 70.7 %copy-start.47 = (f32[1536]{0:T(1024)S(1)}, f32[1536]{0:T(1024)}, u32[]{:S(2)}) copy-start(f32[1536]{0:T(1024)} %copy-done.46) | copy-start | bytes 18436
  950.2 3.4 copy-start.42
  950.2 4.4 copy-start.41
  954.6 4.3 copy-start.21
  955.9 6.2 slice-start.4
  958.9 3.4 slice-start.5
  958.9 7.0 slice-start.2
  962.4 4.6 slice-start.3
  967.0 4.2 copy-start.1
  (23 other events, 41.7 us)
Sparse Core Ops, SparseCore 0:
  22.7 29.8 all-gather.3
  81.3 94.6 all-reduce.6
  198.8 93.6 all-reduce.8
  294.5 165.7 all-gather.5
  536.6 91.8 all-reduce.10
  634.8 315.3 all-reduce.12
